TPU v7x, 256 devices: a whole 4x4x8 slice. The times are simulated.
256 devices in a mesh: row: 8 (over z), col: 8 (over y, core), depth: 4 (over x).
Axes of the slice: x: 4, y: 4, z: 8, core: 2. Of those that a mesh axis runs over, the one named last changes fastest.
Arguments:
- a21_leaf: float32 [4, 4096, 2048], P('depth', 'row', 'col'), may hold values from -1.2 to 1.2
- a12_leaf: float32 [4, 2048, 4096], P('depth', 'row', 'col'), may hold values from -1.2 to 1.2
- uinv_leaf: float32 [4, 2048, 2048], P('depth', None, 'col'), may hold values from -0.2 to 1.5, as said below
- linv_leaf: float32 [4, 2048, 2048], P('depth', 'row'), may hold values from -0.2 to 1.5, as said below
- live: int32 [4], P('depth'), may hold values from 16 to 32
- row_map: int32 [4, 32], P('depth', 'row'), may hold values from 0 to 63, as said below
- col_map: int32 [4, 32], P('depth', 'col'), may hold values from 0 to 63, as said below
- a22_anc: float32 [8192, 8192], P(('row', 'depth'), 'col'), may hold values from -6 to 6
- a21_anc: float32 [8192, 2048], P(('row', 'depth'), 'col'), may hold values from -1.2 to 1.2
- a12_anc: float32 [2048, 8192], P(('row', 'depth'), 'col'), may hold values from -1.2 to 1.2
- uinv_anc: float32 [2048, 2048], P(None, 'col'), may hold values from -0.2 to 1.5, as said below
- linv_anc: float32 [2048, 2048], P(('row', 'depth')), may hold values from -0.2 to 1.5, as said below
Outputs:
- leaf_lower: float32 [4, 4096, 2048], P('depth', 'row', 'col')
- leaf_upper: float32 [4, 2048, 4096], P('depth', 'row', 'col')
- anc_lower: float32 [8192, 2048], P(('row', 'depth'), 'col')
- anc_upper: float32 [2048, 8192], P(('row', 'depth'), 'col')
- anc_schur: float32 [8192, 8192], P(('row', 'depth'), 'col')
Inputs may be any that keep to these rules, and one draw needn't show every extreme that they name: `uinv_leaf`: upper triangular: zero below the diagonal, diagonal between 0.5 and 1.5. `linv_leaf`: lower triangular: zero above the diagonal, diagonal between 0.5 and 1.5. `uinv_anc`: upper triangular: zero below the diagonal, diagonal between 0.5 and 1.5. `linv_anc`: lower triangular: zero above the diagonal, diagonal between 0.5 and 1.5. `row_map`: within one replica the entries are distinct. Leaf block row i lies in the k-th of 8 equal ranges of leaf block rows, and its target lies in the k-th of 8 equal ranges of the 64 ancestor block rows. `col_map`: within one replica the entries are distinct. Leaf block column j lies in the k-th of 8 equal ranges of leaf block columns, and its target lies in the k-th of 8 equal ranges of the 64 ancestor block columns.
All inputs are finite; a program needn't handle non-finite values.
Results may differ from a plain program's by a relative error of at most 0.0001.
Values sent between devices are 32-bit elements; how exact they have to be, the bound alone decides.
No kernel may reach another device: no remote copies, remote signals or barrier semaphores. Data moves between devices by JAX's collectives and lax.ppermute only.
A program may use at most 128 MiB of HBM per device.

v0:
```python
import math
import jax
import jax.numpy as jnp
from jax import lax
from jax.sharding import PartitionSpec as P

NB = 128


def in_one_piece(arrays, axis, split_dim, concat_dim, along):
    widths = [math.prod(a.shape[along:]) for a in arrays]
    both = jnp.concatenate(
        [a.reshape(*a.shape[:along], w) for a, w in zip(arrays, widths)], axis=along
    )
    out = lax.all_to_all(both, axis, split_axis=split_dim, concat_axis=concat_dim, tiled=True)
    tiles = jnp.split(out, [sum(widths[:k]) for k in range(1, len(widths))], axis=along)
    return tuple((b.reshape(*out.shape[:along], *a.shape[along:]) for a, b in zip(arrays, tiles)))


def sent_to_all(shard, axis):
    copies = jnp.broadcast_to(shard, (lax.axis_size(axis), *shard.shape))
    return lax.all_to_all(copies, axis, split_axis=0, concat_axis=0, tiled=True)


def in_order(tiles, dim):
    lengths = list(tiles.shape[1:])
    lengths[dim] *= tiles.shape[0]
    return jnp.moveaxis(tiles, 0, dim).reshape(lengths)


def collect(shard, axis, dim):
    tiles = sent_to_all(shard, axis)
    return in_order(tiles, dim)


def gather_axes(shard, axes, dim):
    out = shard
    for number in range(len(axes) - 1, -1, -1):
        out = lax.all_gather(out, axes[number], axis=dim, tiled=True)
    return out


def product(left, right):
    return jnp.dot(left, right, precision=lax.Precision.HIGHEST, preferred_element_type=jnp.float32)


def combine_depth(schur, row_map, col_map, a22_anc):
    block_size = NB
    rows_here = schur.shape[0]
    cols_here = schur.shape[1]
    leaf_rows = rows_here // block_size
    leaf_cols = cols_here // block_size
    anc_rows = a22_anc.shape[0]
    replicas = lax.axis_size("depth")
    anc_row_blocks = anc_rows * replicas // block_size
    anc_col_blocks = a22_anc.shape[1] // block_size
    row_local = row_map[0] - lax.axis_index("row") * anc_row_blocks
    col_local = col_map[0] - lax.axis_index("col") * anc_col_blocks
    owner_blocks = anc_rows // block_size
    slots = min(leaf_rows, owner_blocks)
    owner = row_local // owner_blocks
    earlier = lax.iota(jnp.int32, leaf_rows)[:, None] > lax.iota(jnp.int32, leaf_rows)[None, :]
    same = owner[:, None] == owner[None, :]
    rank = jnp.sum((earlier & same).astype(jnp.int32), axis=1)
    select = (
        (owner[:, None, None] == lax.iota(jnp.int32, replicas)[None, :, None])
        & (rank[:, None, None] == lax.iota(jnp.int32, slots)[None, None, :])
    ).astype(jnp.float32)
    leaf_blocks = schur.reshape(leaf_rows, block_size, cols_here)
    packed = jnp.einsum("iqs,ixc->qsxc", select, leaf_blocks, precision=lax.Precision.HIGHEST)
    packed = packed.reshape(replicas, slots * block_size, cols_here)
    target = (row_local - owner * owner_blocks + 1).astype(jnp.float32)
    tags = jnp.einsum("iqs,i->qs", select, target, precision=lax.Precision.HIGHEST) - 1.0
    col_tags = jnp.broadcast_to(col_local.astype(jnp.float32)[None, :], (replicas, leaf_cols))
    got_rows, got_tags, got_cols = in_one_piece((packed, tags, col_tags), "depth", 0, 0, 1)
    slot_pick = (
        got_tags[:, :, None] == lax.iota(jnp.int32, owner_blocks).astype(jnp.float32)[None, None, :]
    ).astype(jnp.float32)
    column_pick = (
        got_cols[:, :, None]
        == lax.iota(jnp.int32, anc_col_blocks).astype(jnp.float32)[None, None, :]
    ).astype(jnp.float32)
    pieces = got_rows.reshape(replicas, slots, block_size, leaf_cols, block_size)
    sectioned = jnp.einsum("psa,psxjy->paxjy", slot_pick, pieces, precision=lax.Precision.HIGHEST)
    placed = jnp.einsum("paxjy,pjb->axby", sectioned, column_pick, precision=lax.Precision.HIGHEST)
    return placed.reshape(anc_rows, anc_col_blocks * block_size)


def anc_panels(a21_anc, a12_anc, uinv_anc, linv_anc):
    factor = uinv_anc
    anc_lower = product(collect(a21_anc, "col", 1), factor)
    lower_whole = collect(anc_lower, "col", 1)
    factor = linv_anc
    anc_upper = product(factor, lax.all_gather(a12_anc, ("row", "depth"), axis=0, tiled=True))
    return (anc_lower, lower_whole, anc_upper)


def shards(
    a21_leaf,
    a12_leaf,
    uinv_leaf,
    linv_leaf,
    live,
    row_map,
    col_map,
    a22_anc,
    a21_anc,
    a12_anc,
    uinv_anc,
    linv_anc,
):
    block_size = NB
    panel_left = a21_leaf[0]
    panel_top = a12_leaf[0]
    upper_inverse = uinv_leaf[0]
    lower_inverse = linv_leaf[0]
    rows_here = panel_left.shape[0]
    cols_here = panel_top.shape[1]
    live_rows = live[0] * block_size
    row_pos = lax.axis_index("row") * rows_here + lax.iota(jnp.int32, rows_here)
    col_pos = lax.axis_index("col") * cols_here + lax.iota(jnp.int32, cols_here)
    row_keep = (row_pos < live_rows).astype(jnp.float32)
    col_keep = (col_pos < live_rows).astype(jnp.float32)
    factor = upper_inverse
    lower_part = product(lax.all_gather(panel_left, "col", axis=1, tiled=True), factor)
    leaf_lower = lower_part * row_keep[:, None]
    factor = lower_inverse
    upper_part = product(factor, lax.all_gather(panel_top, "row", axis=0, tiled=True))
    leaf_upper = upper_part * col_keep[None, :]
    upper_whole = lax.all_gather(leaf_upper, "row", axis=0, tiled=True)
    factor = upper_whole
    schur = jnp.zeros((rows_here, cols_here), jnp.float32) - product(
        lax.all_gather(leaf_lower, "col", axis=1, tiled=True), factor
    )
    own_update = combine_depth(schur, row_map, col_map, a22_anc)
    anc_lower, lower_whole, anc_upper = anc_panels(a21_anc, a12_anc, uinv_anc, linv_anc)
    factor = lower_whole
    anc_schur = a22_anc + own_update - product(factor, gather_axes(anc_upper, ("row", "depth"), 0))
    return (leaf_lower[None], leaf_upper[None], anc_lower, anc_upper, anc_schur)


def solution(mesh):
    in_specs = (
        P("depth", "row", "col"),
        P("depth", "row", "col"),
        P("depth", None, "col"),
        P("depth", "row", None),
        P("depth"),
        P("depth", "row"),
        P("depth", "col"),
        P(("row", "depth"), "col"),
        P(("row", "depth"), "col"),
        P(("row", "depth"), "col"),
        P(None, "col"),
        P(("row", "depth"), None),
    )
    out_specs = (
        P("depth", "row", "col"),
        P("depth", "row", "col"),
        P(("row", "depth"), "col"),
        P(("row", "depth"), "col"),
        P(("row", "depth"), "col"),
    )
    return jax.shard_map(shards, mesh=mesh, in_specs=in_specs, out_specs=out_specs, check_vma=False)
```

profile of v0, /device:TPU:1, one launch (start us, length us, event | category | flops | bytes accessed | tf_op | source)
XLA Modules:
  0.0 436.7 jit_solution(4254180319421357973)
XLA Ops:
  7.2 0.0 copy-start
  7.2 0.0 all-gather.20.cloned.1.call-start
  7.2 0.7 all-gather.20.cloned.1.call-update
  7.9 0.0 all-gather.22.cloned.1.call-start
  8.0 0.7 all-gather.22.cloned.1.call-update
  8.7 0.0 all-gather.10.cloned.1.call-start
  8.7 0.7 all-gather.10.cloned.1.call-update
  9.4 0.0 all-gather.12.cloned.1.call-start
  10.1 38.6 %all-gather.20.cloned.1.call-done = f32[1,512,2048]{2,1,0:T(8,128)} async-done(((f32[1,512,256]{2,1,0:T(8,128)}), f32[1,512,2048]{2,1,0:T(8,128)}) %all-gather.20.cloned.1.call-update) | async-done | bytes 4194320 | tf_op jit(solution)/shard_map/all_gather | solution.py:125
  48.7 0.0 copy-done
  48.7 6.4 %fusion.10 = f32[512,256]{1,0:T(8,128)} fusion(f32[1,2048,256]{2,1,0:T(8,128)S(1)} %copy-done, f32[1,512,2048]{2,1,0:T(8,128)} %all-gather.20.cloned.1.call-done, f32[512]{0:T(512)S(1)} %fusion.32), kind=kOutput, calls=%fused_computation.13 | convolution fusion | flops 3221356544 | bytes 6817792 | tf_op jit(solution)/shard_map/dot_general | solution.py:44
  55.1 0.0 all-gather.12.cloned.1.call-update
  55.1 0.0 all-gather.14.cloned.1.call-start
  55.2 0.0 copy-start.4
  55.2 49.4 %all-gather.22.cloned.1.call-done = f32[1,2048,512]{2,1,0:T(8,128)} async-done(((f32[1,256,512]{2,1,0:T(8,128)}), f32[1,2048,512]{2,1,0:T(8,128)}) %all-gather.22.cloned.1.call-update) | async-done | bytes 4194320 | tf_op jit(solution)/shard_map/all_gather | solution.py:128
  104.6 7.3 %fusion.15 = f32[256,512]{1,0:T(8,128)} fusion(f32[1,2048,512]{2,1,0:T(8,128)} %all-gather.22.cloned.1.call-done, f32[1,256,2048]{2,1,0:T(8,128)} %param.15, f32[512]{0:T(512)S(1)} %fusion.33), kind=kOutput, calls=%fused_computation.14 | convolution fusion | flops 3221356544 | bytes 6817792 | tf_op jit(solution)/shard_map/dot_general | solution.py:44
  111.9 0.0 all-gather.14.cloned.1.call-update
  112.0 0.0 copy-done.4
  112.0 0.1 copy.29
  112.1 1.5 broadcast_in_dim.16
  113.6 0.0 copy-start.5
  113.6 5.3 %all-to-all-start = ((f32[8,256,256]{1,2,0:T(8,128)}), f32[8,256,256]{1,2,0:T(8,128)S(1)}, u32[]{:S(2)}, u32[]{:S(2)}) async-start(f32[8,256,256]{1,2,0:T(8,128)} %broadcast_in_dim.16), calls=%async_computation | async-start | bytes 4194304 | tf_op jit(solution)/shard_map/all_to_all | solution.py:22
  118.9 0.0 all-gather.16.cloned.1.call-start
  118.9 0.0 copy-done.5
  118.9 0.1 convert_reduce_fusion
  119.0 84.1 %all-gather.10.cloned.1.call-done = f32[2048,1024]{1,0:T(8,128)} async-done(((f32[64,1024]{1,0:T(8,128)}), f32[2048,1024]{1,0:T(8,128)}) %all-gather.10.cloned.1.call-update) | async-done | bytes 8388624 | tf_op jit(solution)/shard_map/all_gather | solution.py:94
  203.1 0.0 copy-done.3
  203.1 8.2 %fusion.51 = f32[64,1024]{1,0:T(8,128)} fusion(f32[64,2048]{1,0:T(8,128)S(1)} %copy-done.3, f32[2048,1024]{1,0:T(8,128)} %all-gather.10.cloned.1.call-done), kind=kOutput, calls=%fused_computation.69 | convolution fusion | flops 1610612736 | bytes 9175040 | tf_op jit(solution)/shard_map/dot_general | solution.py:44
  211.3 0.0 all-gather.16.cloned.1.call-update
  211.4 0.2 all-gather.18.cloned.1.call-start
  211.6 0.1 fusion.27
  211.7 0.1 copy.37
  211.8 0.0 copy-done.6
  211.8 0.1 bitcast_add_fusion.1
  211.9 26.4 %all-gather.12.cloned.1.call-done = f32[512,2048]{1,0:T(8,128)} async-done(((f32[512,256]{1,0:T(8,128)}), f32[512,2048]{1,0:T(8,128)}) %all-gather.12.cloned.1.call-update) | async-done | bytes 4194320 | tf_op jit(solution)/shard_map/all_gather | solution.py:133
  238.3 56.4 %all-gather.14.cloned.1.call-done = f32[2048,512]{1,0:T(8,128)} async-done(((f32[256,512]{1,0:T(8,128)}), f32[2048,512]{1,0:T(8,128)}) %all-gather.14.cloned.1.call-update) | async-done | bytes 4194320 | tf_op jit(solution)/shard_map/all_gather | solution.py:130
  294.7 9.4 %convolution_subtract_fusion = f32[512,512]{1,0:T(8,128)S(1)} fusion(f32[512,2048]{1,0:T(8,128)} %all-gather.12.cloned.1.call-done, f32[2048,512]{1,0:T(8,128)} %all-gather.14.cloned.1.call-done), kind=kOutput, calls=%fused_computation.11 | convolution fusion | flops 6442713088 | bytes 9437184 | tf_op jit(solution)/shard_map/dot_general | solution.py:44
  304.0 3.6 fusion.20
  307.6 12.7 %all-gather.16.cloned.1.call-done = f32[256,1024]{1,0:T(8,128)} async-done(((f32[64,1024]{1,0:T(8,128)}), f32[256,1024]{1,0:T(8,128)}) %all-gather.16.cloned.1.call-update) | async-done | bytes 1048592 | tf_op jit(solution)/shard_map/all_gather | solution.py:39
  320.3 0.0 all-gather.18.cloned.1.call-update
  320.3 3.1 constant_dynamic-update-slice_fusion
  323.4 1.3 dynamic-update-slice.1
  324.7 1.4 dynamic-update-slice.2
  326.0 4.8 %copy.31 = f32[4,1,131078]{2,1,0:T(1,128)} copy(f32[4,1,131078]{2,0,1:T(4,128)} %bitcast.99) | data formatting | bytes 4194496 | tf_op jit(solution)/shard_map/all_to_all | solution.py:15
  330.9 0.0 all-to-all-done
  330.9 4.5 %all-to-all-start.1 = ((f32[4,1,131078]{2,1,0:T(1,128)}), f32[4,1,131078]{2,1,0:T(1,128)}, u32[]{:S(2)}, u32[]{:S(2)}) async-start(f32[4,1,131078]{2,1,0:T(1,128)} %copy.31), calls=%async_computation.1 | async-start | bytes 4198400 | tf_op jit(solution)/shard_map/all_to_all | solution.py:15
  335.4 5.3 %fusion.50 = f32[256,256]{1,0:T(8,128)S(1)} fusion(f32[256,2048]{0,1:T(8,128)S(1)} %bitcast.100, f32[2048,256]{1,0:T(8,128)} %param.22), kind=kOutput, calls=%fused_computation.68 | convolution fusion | flops 1610612736 | bytes 4456448 | tf_op jit(solution)/shard_map/dot_general | solution.py:44
  340.7 0.0 copy-start.2
  340.7 0.1 copy.35
  340.8 18.3 %all-to-all-done.1 = f32[4,1,131078]{2,1,0:T(1,128)} async-done(((f32[4,1,131078]{2,1,0:T(1,128)}), f32[4,1,131078]{2,1,0:T(1,128)}, u32[]{:S(2)}, u32[]{:S(2)}) %all-to-all-start.1) | async-done | bytes 2097280 | tf_op jit(solution)/shard_map/all_to_all | solution.py:15
  359.1 1.5 broadcast_in_dim.20
  360.6 0.0 copy-done.2
  360.6 7.9 %all-to-all-start.2 = ((f32[8,256,256]{1,2,0:T(8,128)}), f32[8,256,256]{1,2,0:T(8,128)}, u32[]{:S(2)}, u32[]{:S(2)}) async-start(f32[8,256,256]{1,2,0:T(8,128)} %broadcast_in_dim.20), calls=%async_computation.2 | async-start | bytes 4194304 | tf_op jit(solution)/shard_map/all_to_all | solution.py:22
  368.5 2.6 copy.53
  371.2 1.5 split.14
  372.7 0.1 split.12
  372.8 3.4 reshape_reshape.7
  376.2 0.1 copy.32
  376.2 4.8 %fusion.8 = f32[4,2,128,4,128]{4,1,3,2,0:T(2,128)S(1)} fusion(f32[4,2,128,4,128]{4,3,2,1,0:T(4,128)S(1)} %reshape_reshape.7, f32[4,2]{1,0:T(4,128)S(1)} %split.13, f32[2]{0:T(128)S(1)} %iota_convert_fusion), kind=kOutput, calls=%fused_computation.9 | convolution fusion | flops 12582928 | bytes 4194344 | tf_op jit(solution)/shard_map/psa,psxjy->paxjy/dot_general | solution.py:84
  381.0 3.2 fusion.6
  384.3 10.6 %all-to-all-done.2 = f32[8,256,256]{1,2,0:T(8,128)} async-done(((f32[8,256,256]{1,2,0:T(8,128)}), f32[8,256,256]{1,2,0:T(8,128)}, u32[]{:S(2)}, u32[]{:S(2)}) %all-to-all-start.2) | async-done | bytes 2097184 | tf_op jit(solution)/shard_map/all_to_all | solution.py:22
  394.8 23.6 %all-gather.18.cloned.1.call-done = f32[2048,1024]{1,0:T(8,128)} async-done(((f32[256,1024]{1,0:T(8,128)}), f32[2048,1024]{1,0:T(8,128)}) %all-gather.18.cloned.1.call-update) | async-done | bytes 8388624 | tf_op jit(solution)/shard_map/all_gather | solution.py:39
  418.5 11.4 %convolution_subtract_fusion.1 = f32[256,1024]{1,0:T(8,128)} fusion(f32[256,2048]{0,1:T(8,128)} %bitcast.28, f32[2048,1024]{1,0:T(8,128)} %all-gather.18.cloned.1.call-done, f32[256,1024]{1,0:T(8,128)} %param.19, f32[32,8,8,128]{3,2,1,0:T(8,128)S(1)} %bitcast.103), kind=kOutput, calls=%fused_computation.12 | convolution fusion | flops 6442975232 | bytes 13631488 | tf_op jit(solution)/shard_map/dot_general | solution.py:44
  429.9 0.0 copy-done.1
  (14 shorter events, 0.1 us)
Async XLA Ops:
  7.2 41.5 %copy-start = (f32[1,2048,256]{2,1,0:T(8,128)S(1)}, f32[1,2048,256]{2,1,0:T(8,128)}, u32[]{:S(2)}) copy-start(f32[1,2048,256]{2,1,0:T(8,128)} %param.14) | copy-start | bytes 6291460
  7.2 41.5 %all-gather.20.cloned.1.call-start = ((), (), s32[]{:S(2)}) async-start(), calls=%async_computation.8 | async-start | bytes 4718592 | tf_op jit(solution)/shard_map/all_gather | solution.py:125
  7.9 96.7 %all-gather.22.cloned.1.call-start = ((), (), s32[]{:S(2)}) async-start(), calls=%async_computation.9 | async-start | bytes 4718592 | tf_op jit(solution)/shard_map/all_gather | solution.py:128
  8.7 194.5 %all-gather.10.cloned.1.call-start = ((), (), s32[]{:S(2)}) async-start(), calls=%async_computation.3 | async-start | bytes 8650752 | tf_op jit(solution)/shard_map/all_gather | solution.py:94
  9.4 228.9 %all-gather.12.cloned.1.call-start = ((), (), s32[]{:S(2)}) async-start(), calls=%async_computation.4 | async-start | bytes 4718592 | tf_op jit(solution)/shard_map/all_gather | solution.py:133
  55.1 239.5 %all-gather.14.cloned.1.call-start = ((), (), s32[]{:S(2)}) async-start(), calls=%async_computation.5 | async-start | bytes 4718592 | tf_op jit(solution)/shard_map/all_gather | solution.py:130
  55.2 56.8 %copy-start.4 = (f32[256,256]{1,0:T(8,128)S(1)}, f32[256,256]{1,0:T(8,128)}, u32[]{:S(2)}) copy-start(f32[256,256]{1,0:T(8,128)} %param.20) | copy-start | bytes 786436
  113.6 5.3 %copy-start.5 = (s32[1,4]{1,0:T(1,128)S(1)}, s32[1,4]{1,0:T(1,128)}, u32[]{:S(2)}) copy-start(s32[1,4]{1,0:T(1,128)} %param.17) | copy-start | bytes 52
  113.6 89.5 %copy-start.3 = (f32[64,2048]{1,0:T(8,128)S(1)}, f32[64,2048]{1,0:T(8,128)}, u32[]{:S(2)}) copy-start(f32[64,2048]{1,0:T(8,128)} %param.23) | copy-start | bytes 1572868
  113.6 217.2 %all-to-all-start = ((f32[8,256,256]{1,2,0:T(8,128)}), f32[8,256,256]{1,2,0:T(8,128)S(1)}, u32[]{:S(2)}, u32[]{:S(2)}) async-start(f32[8,256,256]{1,2,0:T(8,128)} %broadcast_in_dim.16), calls=%async_computation | async-start | bytes 4194304 | tf_op jit(solution)/shard_map/all_to_all | solution.py:22
  118.9 201.4 %all-gather.16.cloned.1.call-start = ((), (), s32[]{:S(2)}) async-start(), calls=%async_computation.6 | async-start | bytes 1310720 | tf_op jit(solution)/shard_map/all_gather | solution.py:39
  119.0 92.8 %copy-start.6 = (s32[1,4]{1,0:T(1,128)S(1)}, s32[1,4]{1,0:T(1,128)}, u32[]{:S(2)}) copy-start(s32[1,4]{1,0:T(1,128)} %param.18) | copy-start | bytes 52
  211.4 207.1 %all-gather.18.cloned.1.call-start = ((), (), s32[]{:S(2)}) async-start(), calls=%async_computation.7 | async-start | bytes 9437184 | tf_op jit(solution)/shard_map/all_gather | solution.py:39
  330.9 28.3 %all-to-all-start.1 = ((f32[4,1,131078]{2,1,0:T(1,128)}), f32[4,1,131078]{2,1,0:T(1,128)}, u32[]{:S(2)}, u32[]{:S(2)}) async-start(f32[4,1,131078]{2,1,0:T(1,128)} %copy.31), calls=%async_computation.1 | async-start | bytes 4198400 | tf_op jit(solution)/shard_map/all_to_all | solution.py:15
  340.7 20.0 %copy-start.2 = (f32[256,256]{1,0:T(8,128)}, f32[256,256]{1,0:T(8,128)S(1)}, u32[]{:S(2)}) copy-start(f32[256,256]{1,0:T(8,128)S(1)} %fusion.50) | copy-start | bytes 786436
  360.6 34.2 %all-to-all-start.2 = ((f32[8,256,256]{1,2,0:T(8,128)}), f32[8,256,256]{1,2,0:T(8,128)}, u32[]{:S(2)}, u32[]{:S(2)}) async-start(f32[8,256,256]{1,2,0:T(8,128)} %broadcast_in_dim.20), calls=%async_computation.2 | async-start | bytes 4194304 | tf_op jit(solution)/shard_map/all_to_all | solution.py:22
  418.5 11.4 %copy-start.1 = (f32[1,2048,256]{2,1,0:T(8,128)S(1)}, f32[1,2048,256]{2,1,0:T(8,128)}, u32[]{:S(2)}) copy-start(f32[1,2048,256]{2,1,0:T(8,128)} %param.14) | copy-start | bytes 6291460
Sparse Core Ops, SparseCore 0:
  9.8 38.8 all-gather.19
  50.5 54.1 all-gather.21
  107.2 95.8 all-gather.9
  205.4 32.8 all-gather.11
  240.5 54.1 all-gather.13
  296.9 23.3 all-gather.15
  322.0 96.3 all-gather.17
where the time goes:
time: 437 us
  waiting for transfers between devices  322 us (74%)
  matrix products  59.7 us (14%)
  local copies, waits for them, and re-layouts  21.7 us (5%)
  starting transfers between devices  18.1 us (4%)
  between operations  14.9 us (3%)
    all_gather x1, waiting for transfers between devices, anc_panels(): lax.all_gather(a12_anc, ('row', 'depth'), axis=0, tiled=True)  84.1 us
    all_gather x1, waiting for transfers between devices, shards(): upper_whole = lax.all_gather(leaf_upper, 'row', axis=0, tiled=True)  56.4 us
    all_gather x1, waiting for transfers between devices, shards(): lax.all_gather(panel_top, 'row', axis=0, tiled=True)  49.4 us
    dot_general x6, matrix products, product(): jnp.dot(left, right, precision=lax.Precision.HIGHEST, preferred_element_t...  48 us
    all_gather x1, waiting for transfers between devices, shards(): lax.all_gather(panel_left, 'col', axis=1, tiled=True)  38.6 us
    all_gather x2, waiting for transfers between devices, gather_axes(): out = lax.all_gather(out, axes[number], axis=dim, tiled=True)  36.3 us
    all_gather x1, waiting for transfers between devices, shards(): lax.all_gather(leaf_lower, 'col', axis=1, tiled=True)  26.4 us
    all_to_all x1, waiting for transfers between devices, in_one_piece(): lax.all_to_all(both, axis, split_axis=split_dim, concat_axis=concat_dim,...  18.3 us
  transfers between devices with their start and end apart: 10, of which 9 were waited for; matrix products, arithmetic and copies ran while one was open for 16% of the time, Pallas kernels for 0%

commit v1 on v0

--- a/solution.py
+++ b/solution.py
@@ -3,6 +3,7 @@
 import jax.numpy as jnp
 from jax import lax
 from jax.sharding import PartitionSpec as P
+from jax.lax import axis_index, ppermute, psum
 
 NB = 128
 
@@ -109,6 +110,32 @@
     uinv_anc,
     linv_anc,
 ):
+
+    def move_ratios(m, array_axis):
+        device_axis = "row"
+        y_new, opened, t1 = (
+            psum(1, axis_name=device_axis),
+            axis_index(device_axis),
+            m.shape[array_axis],
+        )
+        all_rows = list(map(lambda at: (at, (at + 1) % y_new), range(y_new)))
+        crops = list(map(lambda at: (at, (at - 1) % y_new), range(y_new)))
+        met_up = jnp.zeros((*m.shape[:array_axis], y_new * t1, *m.shape[array_axis + 1 :]), m.dtype)
+        met_up = lax.dynamic_update_slice_in_dim(met_up, m, opened * t1, axis=array_axis)
+        even = mat_out = m
+        heard = y_new // 2
+        for j0 in range(1, heard + 1):
+            even = ppermute(even, axis_name=device_axis, perm=all_rows)
+            met_up = lax.dynamic_update_slice_in_dim(
+                met_up, even, (opened - j0) % y_new * t1, axis=array_axis
+            )
+            if j0 < y_new - heard:
+                mat_out = ppermute(mat_out, axis_name=device_axis, perm=crops)
+                met_up = lax.dynamic_update_slice_in_dim(
+                    met_up, mat_out, (opened + j0) % y_new * t1, axis=array_axis
+                )
+        return met_up
+
     block_size = NB
     panel_left = a21_leaf[0]
     panel_top = a12_leaf[0]
@@ -125,7 +152,7 @@
     lower_part = product(lax.all_gather(panel_left, "col", axis=1, tiled=True), factor)
     leaf_lower = lower_part * row_keep[:, None]
     factor = lower_inverse
-    upper_part = product(factor, lax.all_gather(panel_top, "row", axis=0, tiled=True))
+    upper_part = product(factor, move_ratios(panel_top, 0))
     leaf_upper = upper_part * col_keep[None, :]
     upper_whole = lax.all_gather(leaf_upper, "row", axis=0, tiled=True)
     factor = upper_whole

time: 437 us -> 387 us (0.89); the launches traced: 437 us -> 382 us
  waiting for transfers between devices: 322 us -> 244 us
  starting transfers between devices: 18.1 us -> 34.3 us
  local copies, waits for them, and re-layouts: 21.7 us -> 27.5 us
    all_gather x1 -> x0, waiting for transfers between devices: 49.4 us -> none  [shards(): lax.all_gather(panel_top, 'row', axis=0, tiled=True)]
    ppermute x0 -> x7, waiting for transfers between devices: none -> 40 us  [the longest x4 40 us: move_ratios(): even = ppermute(even, axis_name=device_axis, perm=all_rows)]
    all_gather x1, waiting for transfers between devices: 38.6 us -> 0.02 us  [shards(): lax.all_gather(panel_left, 'col', axis=1, tiled=True)]
    all_gather x1, waiting for transfers between devices: 84.1 us -> 55.4 us  [anc_panels(): lax.all_gather(a12_anc, ('row', 'depth'), axis=0, tiled=True)]
    ppermute x0 -> x7, starting transfers between devices: none -> 11.7 us  [the longest x3 8.67 us: move_ratios(): mat_out = ppermute(mat_out, axis_name=device_axis, perm=crops)]
    all_gather x1, waiting for transfers between devices: 56.4 us -> 46.2 us  [shards(): upper_whole = lax.all_gather(leaf_upper, 'row', axis=0, tiled=True)]
    all_gather x1, waiting for transfers between devices: 26.4 us -> 36.1 us  [shards(): lax.all_gather(leaf_lower, 'col', axis=1, tiled=True)]
    unnamed x18 -> x27, local copies, waits for them, and re-layouts: 7.18 us -> 8.96 us
  transfers between devices with their start and end apart: 10 -> 16, of which waited for: 9 -> 11; matrix products, arithmetic and copies ran while one was open for 16% -> 20% of each run, Pallas kernels for 0% -> 0%
where the time goes in v1:
time: 387 us; the launch traced here: 382 us
  waiting for transfers between devices  244 us (63%)
  matrix products  61 us (16%)
  starting transfers between devices  34.3 us (9%)
  local copies, waits for them, and re-layouts  27.5 us (7%)
  between operations  15.4 us (4%)
    all_gather x1, waiting for transfers between devices, anc_panels(): lax.all_gather(a12_anc, ('row', 'depth'), axis=0, tiled=True)  55.4 us
    dot_general x6, matrix products, product(): jnp.dot(left, right, precision=lax.Precision.HIGHEST, preferred_element_t...  49.3 us
    all_gather x1, waiting for transfers between devices, shards(): upper_whole = lax.all_gather(leaf_upper, 'row', axis=0, tiled=True)  46.2 us
    ppermute x4, waiting for transfers between devices, move_ratios(): even = ppermute(even, axis_name=device_axis, perm=all_rows)  40 us
    all_gather x2, waiting for transfers between devices, gather_axes(): out = lax.all_gather(out, axes[number], axis=dim, tiled=True)  36.7 us
    all_gather x1, waiting for transfers between devices, shards(): lax.all_gather(leaf_lower, 'col', axis=1, tiled=True)  36.1 us
    all_to_all x1, waiting for transfers between devices, in_one_piece(): lax.all_to_all(both, axis, split_axis=split_dim, concat_axis=concat_dim,...  18.3 us
    all_to_all x2, starting transfers between devices, sent_to_all(): return lax.all_to_all(copies, axis, split_axis=0, concat_axis=0, tiled=True)  17.5 us
  transfers between devices with their start and end apart: 16, of which 11 were waited for; matrix products, arithmetic and copies ran while one was open for 20% of the time, Pallas kernels for 0%

profile of v1, /device:TPU:1, one launch (start us, length us, event | category | flops | bytes accessed | tf_op | source)
XLA Modules:
  0.0 382.1 jit_solution(6569275727245892543)
XLA Ops:
  7.2 0.0 all-gather.18.cloned.1.call-start
  7.2 0.7 all-gather.18.cloned.1.call-update
  7.9 0.0 all-gather.8.cloned.1.call-start
  8.0 0.7 all-gather.8.cloned.1.call-update
  8.7 0.0 all-gather.12.cloned.1.call-start
  8.7 2.5 collective-permute-start
  11.3 4.0 %collective-permute-start.1 = (f32[256,512]{1,0:T(8,128)}, f32[256,512]{1,0:T(8,128)S(1)}, u32[]{:S(2)}, u32[]{:S(2)}) collective-permute-start(f32[256,512]{1,0:T(8,128)} %bitcast.108), channel_id=1, source_target_pairs={{0,224},{32,0},{64,32},{96,64},{128,96},{160,128},{192,160},{224,1... | collective-permute-start | bytes 1572872 | tf_op jit(solution)/shard_map/ppermute | solution.py:133
  15.3 11.7 %collective-permute-done = f32[256,512]{1,0:T(8,128)S(1)} collective-permute-done((f32[256,512]{1,0:T(8,128)}, f32[256,512]{1,0:T(8,128)S(1)}, u32[]{:S(2)}, u32[]{:S(2)}) %collective-permute-start) | collective-permute-done | bytes 524320 | tf_op jit(solution)/shard_map/ppermute | solution.py:128
  27.0 0.8 copy-done.6
  27.8 1.9 collective-permute-start.3
  29.7 10.9 %collective-permute-done.2 = f32[256,512]{1,0:T(8,128)} collective-permute-done((f32[256,512]{1,0:T(8,128)S(1)}, f32[256,512]{1,0:T(8,128)}, u32[]{:S(2)}, u32[]{:S(2)}) %collective-permute-start.2) | collective-permute-done | bytes 524320 | tf_op jit(solution)/shard_map/ppermute | solution.py:128
  41.3 0.5 broadcast_in_dim.17
  41.9 2.8 collective-permute-start.5
  44.7 8.8 %collective-permute-done.4 = f32[256,512]{1,0:T(8,128)} collective-permute-done((f32[256,512]{1,0:T(8,128)}, f32[256,512]{1,0:T(8,128)}, u32[]{:S(2)}, u32[]{:S(2)}) %collective-permute-start.4) | collective-permute-done | bytes 524320 | tf_op jit(solution)/shard_map/ppermute | solution.py:128
  53.5 0.5 collective-permute-start.6
  54.1 1.1 constant_dynamic-update-slice_fusion.5
  55.1 1.1 constant_dynamic-update-slice_fusion.4
  56.2 1.1 constant_dynamic-update-slice_fusion.3
  57.4 8.6 %collective-permute-done.6 = f32[256,512]{1,0:T(8,128)S(1)} collective-permute-done((f32[256,512]{1,0:T(8,128)}, f32[256,512]{1,0:T(8,128)S(1)}, u32[]{:S(2)}, u32[]{:S(2)}) %collective-permute-start.6) | collective-permute-done | bytes 524320 | tf_op jit(solution)/shard_map/ppermute | solution.py:128
  66.0 7.6 %fusion.9 = f32[512,256]{1,0:T(8,128)} fusion(f32[2048,512]{1,0:T(8,128)S(1)} %constant_dynamic-update-slice_fusion.1, f32[1,256,2048]{2,1,0:T(8,128)S(1)} %copy-done, f32[512]{0:T(512)S(1)} %fusion.30), kind=kOutput, calls=%fused_computation.12 | convolution fusion | flops 3221356544 | bytes 6817792 | tf_op jit(solution)/shard_map/dot_general | solution.py:45
  73.6 0.0 all-gather.12.cloned.1.call-update
  73.6 0.0 all-gather.10.cloned.1.call-start
  73.7 0.0 all-gather.18.cloned.1.call-done
  73.7 7.2 %fusion.12 = f32[512,256]{1,0:T(8,128)} fusion(f32[1,2048,256]{2,1,0:T(8,128)} %param.14, f32[1,512,2048]{2,1,0:T(8,128)} %all-gather.18.cloned.1.call-done, f32[512]{0:T(512)S(1)} %fusion.29), kind=kOutput, calls=%fused_computation.13 | convolution fusion | flops 3221356544 | bytes 6817792 | tf_op jit(solution)/shard_map/dot_general | solution.py:45
  80.9 0.0 all-gather.10.cloned.1.call-update
  80.9 0.1 copy.32
  81.1 1.5 broadcast_in_dim.19
  82.6 9.6 %all-to-all-start = ((f32[8,256,256]{1,2,0:T(8,128)}), f32[8,256,256]{1,2,0:T(8,128)S(1)}, u32[]{:S(2)}, u32[]{:S(2)}) async-start(f32[8,256,256]{1,2,0:T(8,128)} %broadcast_in_dim.19), calls=%async_computation | async-start | bytes 4194304 | tf_op jit(solution)/shard_map/all_to_all | solution.py:23
  92.2 0.2 all-gather.14.cloned.1.call-start
  92.5 0.1 convert_reduce_fusion
  92.6 55.4 %all-gather.8.cloned.1.call-done = f32[2048,1024]{1,0:T(8,128)} async-done(((f32[64,1024]{1,0:T(8,128)}), f32[2048,1024]{1,0:T(8,128)}) %all-gather.8.cloned.1.call-update) | async-done | bytes 8388624 | tf_op jit(solution)/shard_map/all_gather | solution.py:95
  148.0 8.2 %fusion.48 = f32[64,1024]{1,0:T(8,128)} fusion(f32[64,2048]{1,0:T(8,128)S(1)} %copy-done.4, f32[2048,1024]{1,0:T(8,128)} %all-gather.8.cloned.1.call-done), kind=kOutput, calls=%fused_computation.76 | convolution fusion | flops 1610612736 | bytes 9175040 | tf_op jit(solution)/shard_map/dot_general | solution.py:45
  156.2 0.0 all-gather.14.cloned.1.call-update
  156.2 0.0 all-gather.16.cloned.1.call-start
  156.3 0.1 fusion.24
  156.4 0.1 copy.41
  156.5 0.1 bitcast_add_fusion.1
  156.6 46.2 %all-gather.12.cloned.1.call-done = f32[2048,512]{0,1:T(8,128)} async-done(((f32[256,512]{0,1:T(8,128)}), f32[2048,512]{0,1:T(8,128)}) %all-gather.12.cloned.1.call-update) | async-done | bytes 4194320 | tf_op jit(solution)/shard_map/all_gather | solution.py:157
  202.8 36.1 %all-gather.10.cloned.1.call-done = f32[512,2048]{1,0:T(8,128)} async-done(((f32[512,256]{1,0:T(8,128)}), f32[512,2048]{1,0:T(8,128)}) %all-gather.10.cloned.1.call-update) | async-done | bytes 4194320 | tf_op jit(solution)/shard_map/all_gather | solution.py:160
  238.9 9.4 %convolution_subtract_fusion = f32[512,512]{1,0:T(8,128)S(1)} fusion(f32[512,2048]{1,0:T(8,128)} %all-gather.10.cloned.1.call-done, f32[2048,512]{0,1:T(8,128)} %all-gather.12.cloned.1.call-done), kind=kOutput, calls=%fused_computation.10 | convolution fusion | flops 6442713088 | bytes 9437184 | tf_op jit(solution)/shard_map/dot_general | solution.py:45
  248.3 3.6 fusion.17
  251.9 13.4 %all-gather.14.cloned.1.call-done = f32[256,1024]{1,0:T(8,128)} async-done(((f32[64,1024]{1,0:T(8,128)}), f32[256,1024]{1,0:T(8,128)}) %all-gather.14.cloned.1.call-update) | async-done | bytes 1048592 | tf_op jit(solution)/shard_map/all_gather | solution.py:40
  265.3 0.0 all-gather.16.cloned.1.call-update
  265.3 3.1 constant_dynamic-update-slice_fusion
  268.4 1.3 dynamic-update-slice.1
  269.7 1.4 dynamic-update-slice.2
  271.1 4.8 %copy.34 = f32[4,1,131078]{2,1,0:T(1,128)} copy(f32[4,1,131078]{2,0,1:T(4,128)} %bitcast.99) | data formatting | bytes 4194496 | tf_op jit(solution)/shard_map/all_to_all | solution.py:16
  275.9 4.7 %all-to-all-start.1 = ((f32[4,1,131078]{2,1,0:T(1,128)}), f32[4,1,131078]{2,1,0:T(1,128)}, u32[]{:S(2)}, u32[]{:S(2)}) async-start(f32[4,1,131078]{2,1,0:T(1,128)} %copy.34), calls=%async_computation.1 | async-start | bytes 4198400 | tf_op jit(solution)/shard_map/all_to_all | solution.py:16
  280.6 5.3 %fusion.47 = f32[256,256]{1,0:T(8,128)S(1)} fusion(f32[256,2048]{0,1:T(8,128)S(1)} %bitcast.100, f32[2048,256]{1,0:T(8,128)} %param.22), kind=kOutput, calls=%fused_computation.75 | convolution fusion | flops 1610612736 | bytes 4456448 | tf_op jit(solution)/shard_map/dot_general | solution.py:45
  285.9 0.1 copy.38
  286.0 18.3 %all-to-all-done.1 = f32[4,1,131078]{2,1,0:T(1,128)} async-done(((f32[4,1,131078]{2,1,0:T(1,128)}), f32[4,1,131078]{2,1,0:T(1,128)}, u32[]{:S(2)}, u32[]{:S(2)}) %all-to-all-start.1) | async-done | bytes 2097280 | tf_op jit(solution)/shard_map/all_to_all | solution.py:16
  304.3 1.5 broadcast_in_dim.23
  305.8 7.9 %all-to-all-start.2 = ((f32[8,256,256]{1,2,0:T(8,128)}), f32[8,256,256]{1,2,0:T(8,128)}, u32[]{:S(2)}, u32[]{:S(2)}) async-start(f32[8,256,256]{1,2,0:T(8,128)} %broadcast_in_dim.23), calls=%async_computation.2 | async-start | bytes 4194304 | tf_op jit(solution)/shard_map/all_to_all | solution.py:23
  313.7 1.0 copy.39
  314.7 2.6 copy.57
  317.4 1.5 split.14
  318.9 0.1 split.12
  319.0 3.4 reshape_reshape.7
  322.4 0.1 copy.35
  322.5 4.8 %fusion.7 = f32[4,2,128,4,128]{4,1,3,2,0:T(2,128)S(1)} fusion(f32[4,2,128,4,128]{4,3,2,1,0:T(4,128)S(1)} %reshape_reshape.7, f32[4,2]{1,0:T(4,128)S(1)} %split.13, f32[2]{0:T(128)S(1)} %iota_convert_fusion), kind=kOutput, calls=%fused_computation.8 | convolution fusion | flops 12582928 | bytes 4194344 | tf_op jit(solution)/shard_map/psa,psxjy->paxjy/dot_general | solution.py:85
  327.3 3.2 fusion.5
  330.5 9.6 %all-to-all-done.2 = f32[8,256,256]{1,2,0:T(8,128)} async-done(((f32[8,256,256]{1,2,0:T(8,128)}), f32[8,256,256]{1,2,0:T(8,128)}, u32[]{:S(2)}, u32[]{:S(2)}) %all-to-all-start.2) | async-done | bytes 2097184 | tf_op jit(solution)/shard_map/all_to_all | solution.py:23
  340.0 23.3 %all-gather.16.cloned.1.call-done = f32[2048,1024]{1,0:T(8,128)} async-done(((f32[256,1024]{1,0:T(8,128)}), f32[2048,1024]{1,0:T(8,128)}) %all-gather.16.cloned.1.call-update) | async-done | bytes 8388624 | tf_op jit(solution)/shard_map/all_gather | solution.py:40
  363.3 11.7 %convolution_subtract_fusion.1 = f32[256,1024]{1,0:T(8,128)} fusion(f32[256,2048]{0,1:T(8,128)} %bitcast.29, f32[2048,1024]{1,0:T(8,128)} %all-gather.16.cloned.1.call-done, f32[256,1024]{1,0:T(8,128)} %param.19, f32[32,8,8,128]{3,2,1,0:T(8,128)S(1)} %bitcast.105), kind=kOutput, calls=%fused_computation.11 | convolution fusion | flops 6442975232 | bytes 13631488 | tf_op jit(solution)/shard_map/dot_general | solution.py:45
  (43 shorter events, 0.3 us)
Async XLA Ops:
  7.2 58.8 %copy-start = (f32[1,256,2048]{2,1,0:T(8,128)S(1)}, f32[1,256,2048]{2,1,0:T(8,128)}, u32[]{:S(2)}) copy-start(f32[1,256,2048]{2,1,0:T(8,128)} %param.15) | copy-start | bytes 6291460
  7.2 34.6 %copy-start.5 = (f32[1,256,512]{2,1,0:T(8,128)S(1)}, f32[1,256,512]{2,1,0:T(8,128)}, u32[]{:S(2)}) copy-start(f32[1,256,512]{2,1,0:T(8,128)} %param.13) | copy-start | bytes 1572868
  7.2 66.5 %all-gather.18.cloned.1.call-start = ((), (), s32[]{:S(2)}) async-start(), calls=%async_computation.8 | async-start | bytes 4718592 | tf_op jit(solution)/shard_map/all_gather | solution.py:152
  7.9 140.1 %all-gather.8.cloned.1.call-start = ((), (), s32[]{:S(2)}) async-start(), calls=%async_computation.3 | async-start | bytes 8650752 | tf_op jit(solution)/shard_map/all_gather | solution.py:95
  8.7 194.1 %all-gather.12.cloned.1.call-start = ((), (), s32[]{:S(2)}) async-start(), calls=%async_computation.5 | async-start | bytes 4718592 | tf_op jit(solution)/shard_map/all_gather | solution.py:157
  8.7 18.3 %collective-permute-start = (f32[256,512]{1,0:T(8,128)}, f32[256,512]{1,0:T(8,128)S(1)}, u32[]{:S(2)}, u32[]{:S(2)}) collective-permute-start(f32[256,512]{1,0:T(8,128)} %bitcast.107), channel_id=1, source_target_pairs={{0,32},{32,64},{64,96},{96,128},{128,160},{160,192},{192,224},{224... | collective-permute-start | bytes 1572872 | tf_op jit(solution)/shard_map/ppermute | solution.py:128
  11.3 15.8 %collective-permute-start.1 = (f32[256,512]{1,0:T(8,128)}, f32[256,512]{1,0:T(8,128)S(1)}, u32[]{:S(2)}, u32[]{:S(2)}) collective-permute-start(f32[256,512]{1,0:T(8,128)} %bitcast.108), channel_id=1, source_target_pairs={{0,224},{32,0},{64,32},{96,64},{128,96},{160,128},{192,160},{224,1... | collective-permute-start | bytes 1572872 | tf_op jit(solution)/shard_map/ppermute | solution.py:133
  27.0 0.8 copy-start.6
  27.0 13.5 %collective-permute-start.2 = (f32[256,512]{1,0:T(8,128)S(1)}, f32[256,512]{1,0:T(8,128)}, u32[]{:S(2)}, u32[]{:S(2)}) collective-permute-start(f32[256,512]{1,0:T(8,128)S(1)} %collective-permute-done), channel_id=1, source_target_pairs={{0,32},{32,64},{64,96},{96,128},{128,160},{160,192},{192,224},{224... | collective-permute-start | bytes 1572872 | tf_op jit(solution)/shard_map/ppermute | solution.py:128
  27.8 14.1 %collective-permute-start.3 = (f32[256,512]{1,0:T(8,128)S(1)}, f32[256,512]{1,0:T(8,128)}, u32[]{:S(2)}, u32[]{:S(2)}) collective-permute-start(f32[256,512]{1,0:T(8,128)S(1)} %collective-permute-done.1), channel_id=1, source_target_pairs={{0,224},{32,0},{64,32},{96,64},{128,96},{160,128},{192,160},{224,1... | collective-permute-start | bytes 1572872 | tf_op jit(solution)/shard_map/ppermute | solution.py:133
  40.6 12.9 %collective-permute-start.4 = (f32[256,512]{1,0:T(8,128)}, f32[256,512]{1,0:T(8,128)}, u32[]{:S(2)}, u32[]{:S(2)}) collective-permute-start(f32[256,512]{1,0:T(8,128)} %collective-permute-done.2), channel_id=1, source_target_pairs={{0,32},{32,64},{64,96},{96,128},{128,160},{160,192},{192,224},{224... | collective-permute-start | bytes 1572872 | tf_op jit(solution)/shard_map/ppermute | solution.py:128
  41.3 3.4 copy-start.7
  41.9 15.4 %collective-permute-start.5 = (f32[256,512]{1,0:T(8,128)}, f32[256,512]{1,0:T(8,128)S(1)}, u32[]{:S(2)}, u32[]{:S(2)}) collective-permute-start(f32[256,512]{1,0:T(8,128)} %collective-permute-done.3), channel_id=1, source_target_pairs={{0,224},{32,0},{64,32},{96,64},{128,96},{160,128},{192,160},{224,1... | collective-permute-start | bytes 1572872 | tf_op jit(solution)/shard_map/ppermute | solution.py:133
  53.5 12.4 %collective-permute-start.6 = (f32[256,512]{1,0:T(8,128)}, f32[256,512]{1,0:T(8,128)S(1)}, u32[]{:S(2)}, u32[]{:S(2)}) collective-permute-start(f32[256,512]{1,0:T(8,128)} %collective-permute-done.4), channel_id=1, source_target_pairs={{0,32},{32,64},{64,96},{96,128},{128,160},{160,192},{192,224},{224... | collective-permute-start | bytes 1572872 | tf_op jit(solution)/shard_map/ppermute | solution.py:128
  73.6 7.3 %copy-start.8 = (f32[256,256]{1,0:T(8,128)S(1)}, f32[256,256]{1,0:T(8,128)}, u32[]{:S(2)}) copy-start(f32[256,256]{1,0:T(8,128)} %param.20) | copy-start | bytes 786436
  73.6 165.3 %all-gather.10.cloned.1.call-start = ((), (), s32[]{:S(2)}) async-start(), calls=%async_computation.4 | async-start | bytes 4718592 | tf_op jit(solution)/shard_map/all_gather | solution.py:160
  80.9 11.5 %copy-start.9 = (s32[1,4]{1,0:T(1,128)S(1)}, s32[1,4]{1,0:T(1,128)}, u32[]{:S(2)}) copy-start(s32[1,4]{1,0:T(1,128)} %param.17) | copy-start | bytes 52
  80.9 67.1 %copy-start.4 = (f32[64,2048]{1,0:T(8,128)S(1)}, f32[64,2048]{1,0:T(8,128)}, u32[]{:S(2)}) copy-start(f32[64,2048]{1,0:T(8,128)} %param.23) | copy-start | bytes 1572868
  82.6 193.3 %all-to-all-start = ((f32[8,256,256]{1,2,0:T(8,128)}), f32[8,256,256]{1,2,0:T(8,128)S(1)}, u32[]{:S(2)}, u32[]{:S(2)}) async-start(f32[8,256,256]{1,2,0:T(8,128)} %broadcast_in_dim.19), calls=%async_computation | async-start | bytes 4194304 | tf_op jit(solution)/shard_map/all_to_all | solution.py:23
  92.2 173.0 %all-gather.14.cloned.1.call-start = ((), (), s32[]{:S(2)}) async-start(), calls=%async_computation.6 | async-start | bytes 1310720 | tf_op jit(solution)/shard_map/all_gather | solution.py:40
  92.6 64.0 %copy-start.10 = (s32[1,4]{1,0:T(1,128)S(1)}, s32[1,4]{1,0:T(1,128)}, u32[]{:S(2)}) copy-start(s32[1,4]{1,0:T(1,128)} %param.18) | copy-start | bytes 52
  156.2 207.1 %all-gather.16.cloned.1.call-start = ((), (), s32[]{:S(2)}) async-start(), calls=%async_computation.7 | async-start | bytes 9437184 | tf_op jit(solution)/shard_map/all_gather | solution.py:40
  275.9 28.4 %all-to-all-start.1 = ((f32[4,1,131078]{2,1,0:T(1,128)}), f32[4,1,131078]{2,1,0:T(1,128)}, u32[]{:S(2)}, u32[]{:S(2)}) async-start(f32[4,1,131078]{2,1,0:T(1,128)} %copy.34), calls=%async_computation.1 | async-start | bytes 4198400 | tf_op jit(solution)/shard_map/all_to_all | solution.py:16
  285.9 31.5 %copy-start.3 = (f32[256,256]{1,0:T(8,128)}, f32[256,256]{1,0:T(8,128)S(1)}, u32[]{:S(2)}) copy-start(f32[256,256]{1,0:T(8,128)S(1)} %fusion.47) | copy-start | bytes 786436
  285.9 27.9 %copy-start.2 = (f32[512,256]{1,0:T(8,128)S(1)}, f32[512,256]{1,0:T(8,128)}, u32[]{:S(2)}) copy-start(f32[512,256]{1,0:T(8,128)} %fusion.9) | copy-start | bytes 1572868
  305.8 34.2 %all-to-all-start.2 = ((f32[8,256,256]{1,2,0:T(8,128)}), f32[8,256,256]{1,2,0:T(8,128)}, u32[]{:S(2)}, u32[]{:S(2)}) async-start(f32[8,256,256]{1,2,0:T(8,128)} %broadcast_in_dim.23), calls=%async_computation.2 | async-start | bytes 4194304 | tf_op jit(solution)/shard_map/all_to_all | solution.py:23
  363.3 11.7 %copy-start.1 = (f32[1,256,2048]{2,1,0:T(8,128)S(1)}, f32[1,256,2048]{2,1,0:T(8,128)}, u32[]{:S(2)}) copy-start(f32[1,256,2048]{2,1,0:T(8,128)} %param.15) | copy-start | bytes 6291460
Sparse Core Ops, SparseCore 0:
  9.8 38.8 all-gather.17
  51.3 96.6 all-gather.7
  150.4 52.4 all-gather.11
  205.1 33.7 all-gather.9
  241.1 24.0 all-gather.13
  266.9 96.3 all-gather.15
